TPU v7x, 128 devices: a whole 4x4x4 slice. The times are simulated.
128 devices in a mesh: dp: 8 (over x, core), rollout: 16 (over y, z).
Axes of the slice: x: 4, y: 4, z: 4, core: 2. Of those that a mesh axis runs over, the one named last changes fastest.
Arguments:
- queries: bfloat16 [128, 512, 2560], P(('dp', 'rollout')), may hold values from -100 to 100
- resp_keys: bfloat16 [128, 512, 512], P(('dp', 'rollout')), may hold values from -5 to 5
- resp_values: bfloat16 [128, 512, 512], P(('dp', 'rollout')), may hold values from -6 to 6
- prompt_keys: bfloat16 [8, 256, 512], P('dp', 'rollout'), may hold values from -6 to 6
- prompt_values: bfloat16 [8, 256, 512], P('dp', 'rollout'), may hold values from -6 to 6
- d_out: bfloat16 [128, 512, 2560], P(('dp', 'rollout')), may hold values from -6 to 6
- lengths: int32 [128], replicated, may hold values from 64 to 512
- owner: int32 [128], replicated, may hold values from 0 to 7
Outputs:
- attn_out: bfloat16 [128, 512, 2560], P(('dp', 'rollout'))
- d_queries: bfloat16 [128, 512, 2560], P(('dp', 'rollout'))
- d_resp_keys: bfloat16 [128, 512, 512], P(('dp', 'rollout'))
- d_resp_values: bfloat16 [128, 512, 512], P(('dp', 'rollout'))
- d_prompt_keys: float32 [8, 256, 512], P('dp', 'rollout')
- d_prompt_values: float32 [8, 256, 512], P('dp', 'rollout')
Inputs may be any that keep to these rules, and one draw needn't show every extreme that they name: `lengths`: rows of a block at or past its length are padding.
All inputs are finite; a program needn't handle non-finite values.
Results may differ from a plain program's by a relative error of at most 0.0071.
Values may be sent and summed in bfloat16 or wider, within the bound.
No kernel may reach another device: no remote copies, remote signals or barrier semaphores. Data moves between devices by JAX's collectives and lax.ppermute only.
A program may use at most 128 MiB of HBM per device.

v0:
```python
import jax
import jax.numpy as jnp
from jax import lax
from jax.sharding import PartitionSpec as P

HEAD_DIM = 128
BLOCK = 512
TILE = 128


def cut_along(shard, dim, count):
    dims = shard.shape
    pieces = shard.reshape(*dims[:dim], count, dims[dim] // count, *dims[dim + 1 :])
    return jnp.moveaxis(pieces, dim, 0)


def sent_and_summed(shard, axis, dim):
    pieces = cut_along(shard, dim, lax.axis_size(axis))
    arrived = lax.all_to_all(pieces, axis, split_axis=0, concat_axis=0, tiled=True)
    return arrived.astype(jnp.float32).sum(axis=0)


def attend(q_rows, d_rows, offset, stride, length, keys, values):
    rows = q_rows.shape[0]
    span = keys.shape[0]
    kv_heads = keys.shape[1] // HEAD_DIM
    group = q_rows.shape[1] // keys.shape[1]
    key_heads = keys.reshape(span, kv_heads, HEAD_DIM)
    val_heads = values.reshape(span, kv_heads, HEAD_DIM)
    key_pos = jnp.arange(span, dtype=jnp.int32) - (span - BLOCK)
    live_rows = jnp.clip((length - offset + stride - 1) // stride, 0, rows)
    turns = (live_rows + TILE - 1) // TILE
    scale = HEAD_DIM ** (-0.5)

    def step(turn, carry):
        out_all, dq_all, dk_sum, dv_sum = carry
        start = (turn * TILE).astype(jnp.int32)
        qt = lax.dynamic_slice_in_dim(q_rows, start, TILE, 0).reshape(
            TILE, kv_heads, group, HEAD_DIM
        )
        dt = lax.dynamic_slice_in_dim(d_rows, start, TILE, 0)
        pos = offset + stride * (start + jnp.arange(TILE, dtype=jnp.int32))
        live = pos < length
        dt = jnp.where(live[:, None], dt, jnp.zeros_like(dt)).reshape(
            TILE, kv_heads, group, HEAD_DIM
        )
        scores = (
            jnp.einsum("tkgd,skd->kgts", qt, key_heads, preferred_element_type=jnp.float32) * scale
        )
        allowed = key_pos[None, :] <= pos[:, None]
        scores = jnp.where(allowed, scores, -1e30)
        top = jnp.max(scores, axis=-1, keepdims=True)
        expd = jnp.exp(scores - top)
        probs = expd / jnp.sum(expd, axis=-1, keepdims=True)
        weights = probs.astype(jnp.bfloat16)
        out = jnp.einsum("kgts,skd->tkgd", weights, val_heads, preferred_element_type=jnp.float32)
        out = out * live.astype(jnp.float32)[:, None, None, None]
        dprob = jnp.einsum("tkgd,skd->kgts", dt, val_heads, preferred_element_type=jnp.float32)
        delta = jnp.einsum("tkgd,tkgd->kgt", dt.astype(jnp.float32), out)
        dscore = (probs * (dprob - delta[..., None]) * scale).astype(jnp.bfloat16)
        dq = jnp.einsum("kgts,skd->tkgd", dscore, key_heads, preferred_element_type=jnp.float32)
        dk_sum = dk_sum + jnp.einsum(
            "kgts,tkgd->skd", dscore, qt, preferred_element_type=jnp.float32
        )
        dv_sum = dv_sum + jnp.einsum(
            "kgts,tkgd->skd", weights, dt, preferred_element_type=jnp.float32
        )
        out_all = lax.dynamic_update_slice_in_dim(
            out_all, out.reshape(TILE, -1).astype(jnp.bfloat16), start, 0
        )
        dq_all = lax.dynamic_update_slice_in_dim(
            dq_all, dq.reshape(TILE, -1).astype(jnp.bfloat16), start, 0
        )
        return (out_all, dq_all, dk_sum, dv_sum)

    init = (
        jnp.zeros((rows, q_rows.shape[1]), jnp.bfloat16),
        jnp.zeros((rows, q_rows.shape[1]), jnp.bfloat16),
        jnp.zeros((span, kv_heads, HEAD_DIM), jnp.float32),
        jnp.zeros((span, kv_heads, HEAD_DIM), jnp.float32),
    )
    out_all, dq_all, dk_sum, dv_sum = lax.fori_loop(jnp.int32(0), turns, step, init)
    return (out_all, dq_all, dk_sum.reshape(span, -1), dv_sum.reshape(span, -1))


def block_inputs(whole_prompt, group_index, keys_block, values_block, width_k):
    prompt_pair = lax.dynamic_index_in_dim(whole_prompt, group_index, 0, keepdims=False)
    keys = jnp.concatenate([prompt_pair[:, :width_k], keys_block], axis=0)
    values = jnp.concatenate([prompt_pair[:, width_k:], values_block], axis=0)
    return (keys, values)


def per_device(queries, resp_keys, resp_values, prompt_keys, prompt_values, d_out, lengths, owner):
    rollout_count = lax.axis_size("rollout")
    groups = lax.axis_size("dp")
    row_base = lax.axis_index("dp") * rollout_count
    here = row_base + lax.axis_index("rollout")
    shard_rows = prompt_keys.shape[1]
    prompt_n = shard_rows * rollout_count
    width_k = prompt_keys.shape[2]
    local_pair = jnp.concatenate([prompt_keys[0], prompt_values[0]], axis=1)
    gathered = lax.all_gather(local_pair, ("dp", "rollout"), axis=0, tiled=True)
    whole_prompt = gathered.reshape(groups, prompt_n, 2 * width_k)
    group_ids = jnp.arange(groups, dtype=jnp.int32)
    own_group = owner[here]
    own_keys, own_values = block_inputs(
        whole_prompt, own_group, resp_keys[0], resp_values[0], width_k
    )
    row_owner = lax.dynamic_slice_in_dim(owner, row_base, rollout_count, 0)
    out, dq, dk_all, dv_all = attend(
        queries[0], d_out[0], 0, 1, lengths[here], own_keys, own_values
    )
    dk_resp = dk_all[prompt_n:]
    dv_resp = dv_all[prompt_n:]
    terms = jnp.concatenate([dk_all[:prompt_n], dv_all[:prompt_n]], axis=1)[None]
    source_groups = row_owner[None]
    pieces = terms.reshape(terms.shape[0], rollout_count, shard_rows, 2 * width_k)
    received = lax.all_to_all(
        pieces.astype(jnp.bfloat16), "rollout", split_axis=1, concat_axis=1, tiled=True
    ).astype(pieces.dtype)
    picks = (source_groups[:, :, None] == group_ids[None, None, :]).astype(jnp.float32)
    by_group = jnp.einsum("msg,msrc->grc", picks, received, precision=lax.Precision.HIGHEST)
    summed = sent_and_summed(by_group.astype(jnp.bfloat16), "dp", 0)[0]
    return (
        out[None],
        dq[None],
        dk_resp.astype(jnp.bfloat16)[None],
        dv_resp.astype(jnp.bfloat16)[None],
        summed[None, :, :width_k],
        summed[None, :, width_k:],
    )


def solution(mesh):
    placed = (
        P(("dp", "rollout"), None, None),
        P(("dp", "rollout"), None, None),
        P(("dp", "rollout"), None, None),
        P("dp", "rollout", None),
        P("dp", "rollout", None),
        P(("dp", "rollout"), None, None),
        P(),
        P(),
    )
    return jax.shard_map(
        per_device,
        mesh=mesh,
        in_specs=placed,
        out_specs=(
            P(("dp", "rollout"), None, None),
            P(("dp", "rollout"), None, None),
            P(("dp", "rollout"), None, None),
            P(("dp", "rollout"), None, None),
            P("dp", "rollout", None),
            P("dp", "rollout", None),
        ),
        check_vma=False,
    )
```

profile of v0, /device:TPU:1, one launch (start us, length us, event | category | flops | bytes accessed | tf_op | source)
XLA Modules:
  0.0 223.1 jit_solution(10658430492384995604)
XLA Ops:
  7.2 1.4 pad_maximum_fusion.2
  14.3 2.0 copy.50
  16.4 4.5 %copy.47 = bf16[1,512,2560]{1,2,0:T(8,128)(2,1)} copy(bf16[1,512,2560]{2,1,0:T(8,128)(2,1)} %param.10) | data formatting | bytes 5242880 | tf_op args[0]
  20.9 2.6 %copy.51 = bf16[1,512,2560]{1,2,0:T(8,128)(2,1)} copy(bf16[1,512,2560]{2,1,0:T(8,128)(2,1)S(1)} %copy-done.5) | data formatting | bytes 5242880 | tf_op args[5]
  24.3 57.5 %all-gather.2.cloned.1.call-done = bf16[2048,1024]{1,0:T(8,128)(2,1)} async-done(((bf16[16,1024]{1,0:T(8,128)(2,1)}), bf16[2048,1024]{1,0:T(8,128)(2,1)}) %all-gather.2.cloned.1.call-update) | async-done | bytes 4194320 | tf_op jit(solution)/shard_map/all_gather | solution.py:102
  86.8 1.7 broadcast.73.clone2
  88.4 1.7 broadcast.73.clone
  90.1 95.3 %while.17 = (s32[]{:T(128)}, bf16[512,2560]{1,0:T(8,128)(2,1)}, bf16[512,2560]{1,0:T(8,128)(2,1)}, f32[768,4,128]{0,2,1:T(8,128)}, f32[768,4,128]{0,2,1:T(8,128)...) while((s32[]{:T(128)}, bf16[512,2560]{1,0:T(8,128)(2,1)}, ...), condition=%wide.region_3.4_spmd.clone, body=%wide.region_0.3_spmd.clone.sunk | while | flops 3048635904 | bytes 116517448 | solution.py:82
  90.9 1.5 dynamic-slice_select_fusion.2
  92.3 2.4 %fusion.68 = f32[4,128,5,768]{3,1,2,0:T(8,128)S(1)} fusion(bf16[128,4,5,128]{0,3,2,1:T(8,128)(2,1)S(1)} %bitcast.145, bf16[768,4,128]{0,2,1:T(8,128)(2,1)} %get-tuple-element.278), kind=kOutput, calls=%fused_computation.26.clone.1 | convolution fusion | flops 503316480 | bytes 9306112 | tf_op jit(solution)/shard_map/while/body/tkgd,skd->kgts/dot_general | solution.py:48
  94.7 3.7 %fusion.69 = (f32[4,5,128]{2,1,0:T(8,128)S(1)}, f32[4,5,128,768]{3,2,1,0:T(8,128)S(1)}) fusion(f32[4,128,5,768]{3,1,2,0:T(8,128)S(1)} %fusion.68, pred[128,768]{1,0:T(8,128)(4,1)S(1)} %broadcast_compare_fusion.4), kind=kOutput, calls=%fused_computation.54.clone.1 | output fusion | flops 11797247 | bytes 15837184 | tf_op jit(solution)/shard_map/while/body/sub | solution.py:53
  101.8 3.6 %fusion.72 = bf16[4,5,128,768]{3,2,1,0:T(8,128)(2,1)} fusion(f32[4,5,128]{2,1,0:T(8,128)S(1)} %get-tuple-element.240, f32[4,5,128,768]{3,2,1,0:T(8,128)S(1)} %get-tuple-element.237, f32[4,5,128]{2,1,0:T(8,128)S(1)} %get-tuple-element.238, bf16[128,4,5,128]{0,3,2,1:T(8,128)(2,1)S(1)} %bitcast.149, bf16[768,4,128]{2,0,1:T(8,128)(2,1)S(1)} %copy-done.7), kind=kOutput, calls=%fused_computation.5.clone.1 | convolution fusion | flops 513146880 | bytes 13258752 | tf_op jit(solution)/shard_map/while/body/tkgd,skd->kgts/dot_general | solution.py:58
  105.7 3.7 %convolution_convert_fusion.3 = bf16[4,5,128,128]{2,3,1,0:T(8,128)(2,1)S(1)} fusion(bf16[4,5,128,768]{3,2,1,0:T(8,128)(2,1)} %fusion.72, bf16[768,4,128]{0,2,1:T(8,128)(2,1)} %get-tuple-element.278), kind=kOutput, calls=%fused_computation.19.clone.1 | convolution fusion | flops 503644160 | bytes 5373952 | tf_op jit(solution)/shard_map/while/body/kgts,skd->tkgd/dot_general | solution.py:61
  114.7 1.5 dynamic-slice_select_fusion.2
  116.2 2.4 %fusion.68 = f32[4,128,5,768]{3,1,2,0:T(8,128)S(1)} fusion(bf16[128,4,5,128]{0,3,2,1:T(8,128)(2,1)S(1)} %bitcast.145, bf16[768,4,128]{0,2,1:T(8,128)(2,1)} %get-tuple-element.278), kind=kOutput, calls=%fused_computation.26.clone.1 | convolution fusion | flops 503316480 | bytes 9306112 | tf_op jit(solution)/shard_map/while/body/tkgd,skd->kgts/dot_general | solution.py:48
  118.5 3.7 %fusion.69 = (f32[4,5,128]{2,1,0:T(8,128)S(1)}, f32[4,5,128,768]{3,2,1,0:T(8,128)S(1)}) fusion(f32[4,128,5,768]{3,1,2,0:T(8,128)S(1)} %fusion.68, pred[128,768]{1,0:T(8,128)(4,1)S(1)} %broadcast_compare_fusion.4), kind=kOutput, calls=%fused_computation.54.clone.1 | output fusion | flops 11797247 | bytes 15837184 | tf_op jit(solution)/shard_map/while/body/sub | solution.py:53
  125.7 3.6 %fusion.72 = bf16[4,5,128,768]{3,2,1,0:T(8,128)(2,1)} fusion(f32[4,5,128]{2,1,0:T(8,128)S(1)} %get-tuple-element.240, f32[4,5,128,768]{3,2,1,0:T(8,128)S(1)} %get-tuple-element.237, f32[4,5,128]{2,1,0:T(8,128)S(1)} %get-tuple-element.238, bf16[128,4,5,128]{0,3,2,1:T(8,128)(2,1)S(1)} %bitcast.149, bf16[768,4,128]{2,0,1:T(8,128)(2,1)S(1)} %copy-done.7), kind=kOutput, calls=%fused_computation.5.clone.1 | convolution fusion | flops 513146880 | bytes 13258752 | tf_op jit(solution)/shard_map/while/body/tkgd,skd->kgts/dot_general | solution.py:58
  129.6 3.7 %convolution_convert_fusion.3 = bf16[4,5,128,128]{2,3,1,0:T(8,128)(2,1)S(1)} fusion(bf16[4,5,128,768]{3,2,1,0:T(8,128)(2,1)} %fusion.72, bf16[768,4,128]{0,2,1:T(8,128)(2,1)} %get-tuple-element.278), kind=kOutput, calls=%fused_computation.19.clone.1 | convolution fusion | flops 503644160 | bytes 5373952 | tf_op jit(solution)/shard_map/while/body/kgts,skd->tkgd/dot_general | solution.py:61
  138.5 1.5 dynamic-slice_select_fusion.2
  140.0 2.4 %fusion.68 = f32[4,128,5,768]{3,1,2,0:T(8,128)S(1)} fusion(bf16[128,4,5,128]{0,3,2,1:T(8,128)(2,1)S(1)} %bitcast.145, bf16[768,4,128]{0,2,1:T(8,128)(2,1)} %get-tuple-element.278), kind=kOutput, calls=%fused_computation.26.clone.1 | convolution fusion | flops 503316480 | bytes 9306112 | tf_op jit(solution)/shard_map/while/body/tkgd,skd->kgts/dot_general | solution.py:48
  142.4 3.7 %fusion.69 = (f32[4,5,128]{2,1,0:T(8,128)S(1)}, f32[4,5,128,768]{3,2,1,0:T(8,128)S(1)}) fusion(f32[4,128,5,768]{3,1,2,0:T(8,128)S(1)} %fusion.68, pred[128,768]{1,0:T(8,128)(4,1)S(1)} %broadcast_compare_fusion.4), kind=kOutput, calls=%fused_computation.54.clone.1 | output fusion | flops 11797247 | bytes 15837184 | tf_op jit(solution)/shard_map/while/body/sub | solution.py:53
  149.5 3.6 %fusion.72 = bf16[4,5,128,768]{3,2,1,0:T(8,128)(2,1)} fusion(f32[4,5,128]{2,1,0:T(8,128)S(1)} %get-tuple-element.240, f32[4,5,128,768]{3,2,1,0:T(8,128)S(1)} %get-tuple-element.237, f32[4,5,128]{2,1,0:T(8,128)S(1)} %get-tuple-element.238, bf16[128,4,5,128]{0,3,2,1:T(8,128)(2,1)S(1)} %bitcast.149, bf16[768,4,128]{2,0,1:T(8,128)(2,1)S(1)} %copy-done.7), kind=kOutput, calls=%fused_computation.5.clone.1 | convolution fusion | flops 513146880 | bytes 13258752 | tf_op jit(solution)/shard_map/while/body/tkgd,skd->kgts/dot_general | solution.py:58
  153.4 3.7 %convolution_convert_fusion.3 = bf16[4,5,128,128]{2,3,1,0:T(8,128)(2,1)S(1)} fusion(bf16[4,5,128,768]{3,2,1,0:T(8,128)(2,1)} %fusion.72, bf16[768,4,128]{0,2,1:T(8,128)(2,1)} %get-tuple-element.278), kind=kOutput, calls=%fused_computation.19.clone.1 | convolution fusion | flops 503644160 | bytes 5373952 | tf_op jit(solution)/shard_map/while/body/kgts,skd->tkgd/dot_general | solution.py:61
  162.4 1.5 dynamic-slice_select_fusion.2
  163.8 2.4 %fusion.68 = f32[4,128,5,768]{3,1,2,0:T(8,128)S(1)} fusion(bf16[128,4,5,128]{0,3,2,1:T(8,128)(2,1)S(1)} %bitcast.145, bf16[768,4,128]{0,2,1:T(8,128)(2,1)} %get-tuple-element.278), kind=kOutput, calls=%fused_computation.26.clone.1 | convolution fusion | flops 503316480 | bytes 9306112 | tf_op jit(solution)/shard_map/while/body/tkgd,skd->kgts/dot_general | solution.py:48
  166.2 3.7 %fusion.69 = (f32[4,5,128]{2,1,0:T(8,128)S(1)}, f32[4,5,128,768]{3,2,1,0:T(8,128)S(1)}) fusion(f32[4,128,5,768]{3,1,2,0:T(8,128)S(1)} %fusion.68, pred[128,768]{1,0:T(8,128)(4,1)S(1)} %broadcast_compare_fusion.4), kind=kOutput, calls=%fused_computation.54.clone.1 | output fusion | flops 11797247 | bytes 15837184 | tf_op jit(solution)/shard_map/while/body/sub | solution.py:53
  173.3 3.6 %fusion.72 = bf16[4,5,128,768]{3,2,1,0:T(8,128)(2,1)} fusion(f32[4,5,128]{2,1,0:T(8,128)S(1)} %get-tuple-element.240, f32[4,5,128,768]{3,2,1,0:T(8,128)S(1)} %get-tuple-element.237, f32[4,5,128]{2,1,0:T(8,128)S(1)} %get-tuple-element.238, bf16[128,4,5,128]{0,3,2,1:T(8,128)(2,1)S(1)} %bitcast.149, bf16[768,4,128]{2,0,1:T(8,128)(2,1)S(1)} %copy-done.7), kind=kOutput, calls=%fused_computation.5.clone.1 | convolution fusion | flops 513146880 | bytes 13258752 | tf_op jit(solution)/shard_map/while/body/tkgd,skd->kgts/dot_general | solution.py:58
  177.2 3.7 %convolution_convert_fusion.3 = bf16[4,5,128,128]{2,3,1,0:T(8,128)(2,1)S(1)} fusion(bf16[4,5,128,768]{3,2,1,0:T(8,128)(2,1)} %fusion.72, bf16[768,4,128]{0,2,1:T(8,128)(2,1)} %get-tuple-element.278), kind=kOutput, calls=%fused_computation.19.clone.1 | convolution fusion | flops 503644160 | bytes 5373952 | tf_op jit(solution)/shard_map/while/body/kgts,skd->tkgd/dot_general | solution.py:61
  188.4 3.7 %all-to-all-start = ((bf16[1,16,16,1024]{3,2,0,1:T(8,128)(2,1)}), bf16[1,16,16,1024]{3,2,0,1:T(8,128)(2,1)S(1)}, u32[]{:S(2)}, u32[]{:S(2)}) async-start(bf16[1,16,16,1024]{3,2,0,1:T(8,128)(2,1)} %maximum_bitcast_fusion), calls=%async_computation | async-start | bytes 1048576 | tf_op jit(solution)/shard_map/all_to_all | solution.py:118
  192.2 10.4 %all-to-all-done = bf16[1,16,16,1024]{3,2,0,1:T(8,128)(2,1)S(1)} async-done(((bf16[1,16,16,1024]{3,2,0,1:T(8,128)(2,1)}), bf16[1,16,16,1024]{3,2,0,1:T(8,128)(2,1)S(1)}, u32[]{:S(2)}, u32[]{:S(2)}) %all-to-all-start) | async-done | bytes 524320 | tf_op jit(solution)/shard_map/all_to_all | solution.py:118
  203.9 5.2 %all-to-all-start.1 = ((bf16[8,1,16,1024]{3,2,1,0:T(8,128)(2,1)}), bf16[8,1,16,1024]{3,2,1,0:T(8,128)(2,1)S(1)}, u32[]{:S(2)}, u32[]{:S(2)}) async-start(bf16[8,1,16,1024]{3,2,1,0:T(8,128)(2,1)} %copy.61), calls=%async_computation.1 | async-start | bytes 524288 | tf_op jit(solution)/shard_map/all_to_all | solution.py:19
  211.1 4.4 %all-to-all-done.1 = bf16[8,1,16,1024]{3,2,1,0:T(8,128)(2,1)S(1)} async-done(((bf16[8,1,16,1024]{3,2,1,0:T(8,128)(2,1)}), bf16[8,1,16,1024]{3,2,1,0:T(8,128)(2,1)S(1)}, u32[]{:S(2)}, u32[]{:S(2)}) %all-to-all-start.1) | async-done | bytes 262176 | tf_op jit(solution)/shard_map/all_to_all | solution.py:19
  (122 shorter events, 51.1 us)
Async XLA Ops:
  7.2 74.6 %all-gather.2.cloned.1.call-start = ((), (), s32[]{:S(2)}) async-start(), calls=%async_computation.2 | async-start | bytes 4227072 | tf_op jit(solution)/shard_map/all_gather | solution.py:102
  16.4 4.6 %copy-start.5 = (bf16[1,512,2560]{2,1,0:T(8,128)(2,1)S(1)}, bf16[1,512,2560]{2,1,0:T(8,128)(2,1)}, u32[]{:S(2)}) copy-start(bf16[1,512,2560]{2,1,0:T(8,128)(2,1)} %param.15) | copy-start | bytes 7864324
  23.5 59.6 %copy-start.6 = (bf16[1,512,512]{1,2,0:T(8,128)(2,1)S(1)}, bf16[1,512,512]{1,2,0:T(8,128)(2,1)}, u32[]{:S(2)}) copy-start(bf16[1,512,512]{1,2,0:T(8,128)(2,1)} %copy.50) | copy-start | bytes 1572868
  98.4 1.1 copy-start.7
  105.7 3.8 %copy-start = (bf16[4,5,128,768]{3,2,1,0:T(8,128)(2,1)S(1)}, bf16[4,5,128,768]{3,2,1,0:T(8,128)(2,1)}, u32[]{:S(2)}) copy-start(bf16[4,5,128,768]{3,2,1,0:T(8,128)(2,1)} %fusion.72) | copy-start | bytes 11796484 | tf_op jit(solution)/shard_map/while
  105.7 4.0 %copy-start.1 = (f32[768,4,128]{0,2,1:T(8,128)S(1)}, f32[768,4,128]{0,2,1:T(8,128)}, u32[]{:S(2)}) copy-start(f32[768,4,128]{0,2,1:T(8,128)} %get-tuple-element.259) | copy-start | bytes 4718596 | tf_op jit(solution)/shard_map/while
  110.7 1.2 copy-start.2
  122.2 1.1 copy-start.7
  129.6 3.8 %copy-start = (bf16[4,5,128,768]{3,2,1,0:T(8,128)(2,1)S(1)}, bf16[4,5,128,768]{3,2,1,0:T(8,128)(2,1)}, u32[]{:S(2)}) copy-start(bf16[4,5,128,768]{3,2,1,0:T(8,128)(2,1)} %fusion.72) | copy-start | bytes 11796484 | tf_op jit(solution)/shard_map/while
  129.6 4.0 %copy-start.1 = (f32[768,4,128]{0,2,1:T(8,128)S(1)}, f32[768,4,128]{0,2,1:T(8,128)}, u32[]{:S(2)}) copy-start(f32[768,4,128]{0,2,1:T(8,128)} %get-tuple-element.259) | copy-start | bytes 4718596 | tf_op jit(solution)/shard_map/while
  134.6 1.2 copy-start.2
  146.1 1.1 copy-start.7
  153.4 3.8 %copy-start = (bf16[4,5,128,768]{3,2,1,0:T(8,128)(2,1)S(1)}, bf16[4,5,128,768]{3,2,1,0:T(8,128)(2,1)}, u32[]{:S(2)}) copy-start(bf16[4,5,128,768]{3,2,1,0:T(8,128)(2,1)} %fusion.72) | copy-start | bytes 11796484 | tf_op jit(solution)/shard_map/while
  153.4 4.0 %copy-start.1 = (f32[768,4,128]{0,2,1:T(8,128)S(1)}, f32[768,4,128]{0,2,1:T(8,128)}, u32[]{:S(2)}) copy-start(f32[768,4,128]{0,2,1:T(8,128)} %get-tuple-element.259) | copy-start | bytes 4718596 | tf_op jit(solution)/shard_map/while
  158.4 1.2 copy-start.2
  169.9 1.1 copy-start.7
  177.2 3.8 %copy-start = (bf16[4,5,128,768]{3,2,1,0:T(8,128)(2,1)S(1)}, bf16[4,5,128,768]{3,2,1,0:T(8,128)(2,1)}, u32[]{:S(2)}) copy-start(bf16[4,5,128,768]{3,2,1,0:T(8,128)(2,1)} %fusion.72) | copy-start | bytes 11796484 | tf_op jit(solution)/shard_map/while
  177.2 4.0 %copy-start.1 = (f32[768,4,128]{0,2,1:T(8,128)S(1)}, f32[768,4,128]{0,2,1:T(8,128)}, u32[]{:S(2)}) copy-start(f32[768,4,128]{0,2,1:T(8,128)} %get-tuple-element.259) | copy-start | bytes 4718596 | tf_op jit(solution)/shard_map/while
  182.2 1.2 copy-start.2
  185.4 1.7 copy-start.3
  185.5 0.9 copy-start.4
  187.1 5.0 %copy-start.8 = (s32[128]{0:T(128)S(1)}, s32[128]{0:T(128)}, u32[]{:S(2)}) copy-start(s32[128]{0:T(128)} %param.17) | copy-start | bytes 1540
  188.4 20.7 %slice-start = ((bf16[768,4,128]{0,2,1:T(8,128)(2,1)}), bf16[512,4,128]{0,2,1:T(8,128)(2,1)S(1)}, s32[]{:S(2)}) async-start(bf16[768,4,128]{0,2,1:T(8,128)(2,1)} %copy-done.4), calls=%async_computation.3 | async-start | bytes 1048576 | tf_op jit(solution)/shard_map/slice | solution.py:114
  188.4 14.2 %all-to-all-start = ((bf16[1,16,16,1024]{3,2,0,1:T(8,128)(2,1)}), bf16[1,16,16,1024]{3,2,0,1:T(8,128)(2,1)S(1)}, u32[]{:S(2)}, u32[]{:S(2)}) async-start(bf16[1,16,16,1024]{3,2,0,1:T(8,128)(2,1)} %maximum_bitcast_fusion), calls=%async_computation | async-start | bytes 1048576 | tf_op jit(solution)/shard_map/all_to_all | solution.py:118
  203.9 11.7 %all-to-all-start.1 = ((bf16[8,1,16,1024]{3,2,1,0:T(8,128)(2,1)}), bf16[8,1,16,1024]{3,2,1,0:T(8,128)(2,1)S(1)}, u32[]{:S(2)}, u32[]{:S(2)}) async-start(bf16[8,1,16,1024]{3,2,1,0:T(8,128)(2,1)} %copy.61), calls=%async_computation.1 | async-start | bytes 524288 | tf_op jit(solution)/shard_map/all_to_all | solution.py:19
Sparse Core Ops, SparseCore 0:
  11.7 70.0 all-gather.1
where the time goes:
time: 224 us; the launch traced here: 223 us
  waiting for transfers between devices  72.4 us (32%)
  matrix products  52.5 us (23%)
  local copies, waits for them, and re-layouts  42.1 us (19%)
  other arithmetic  29.7 us (13%)
  between operations  16.9 us (8%)
  starting transfers between devices  8.94 us (4%)
    all_gather x1, waiting for transfers between devices, per_device(): gathered = lax.all_gather(local_pair, ('dp', 'rollout'), axis=0, tiled=True)  57.5 us
    dot_general x4, matrix products, step(): jnp.einsum('kgts,skd->tkgd', dscore, key_heads, preferred_element_type=jn...  14.9 us
    sub x4, other arithmetic, step(): expd = jnp.exp(scores - top)  14.7 us
    dot_general x4, matrix products, step(): jnp.einsum('tkgd,skd->kgts', dt, val_heads, preferred_element_type=jnp.fl...  14.5 us
    unnamed x16, local copies, waits for them, and re-layouts  13.2 us
    all_to_all x1, waiting for transfers between devices, per_device(): lax.all_to_all(pieces.astype(jnp.bfloat16), 'rollout', split_axis=1, conc...  10.4 us
    dot_general x4, matrix products, step(): jnp.einsum('tkgd,skd->kgts', qt, key_heads, preferred_element_type=jnp.fl...  9.42 us
    while x32, local copies, waits for them, and re-layouts  7.41 us
  transfers between devices with their start and end apart: 3, of which 3 were waited for; matrix products, arithmetic and copies ran while one was open for 7% of the time, Pallas kernels for 0%

commit v1 on v0

v1 whole, which is shorter than its diff:
```python
import functools

import jax
import jax.numpy as jnp
from jax import lax
from jax.experimental import pallas as pl
from jax.experimental.pallas import tpu as pltpu
from jax.sharding import PartitionSpec as P

HEAD_DIM = 128
ROWS = 256
F32 = jnp.float32
BF16 = jnp.bfloat16
LOG2_E = 1.4426950408889634
ROW_BY_ROW = (((1,), (1,)), ((), ()))


def here_of():
    return lax.axis_index("dp") * lax.axis_size("rollout") + lax.axis_index("rollout")


def select_kernel(owner_ref, groups_ref, out_ref):
    base = lax.axis_index("dp") * lax.axis_size("rollout")
    for r in range(out_ref.shape[0]):
        out_ref[r] = groups_ref[owner_ref[base + r]]


def select_slices(owner, groups, count):
    return pl.pallas_call(
        select_kernel,
        out_shape=jax.ShapeDtypeStruct((count,) + groups.shape[1:], groups.dtype),
        in_specs=[pl.BlockSpec(memory_space=pltpu.SMEM), pl.BlockSpec(memory_space=pltpu.VMEM)],
        out_specs=pl.BlockSpec(memory_space=pltpu.VMEM),
        name="select_slices",
    )(owner, groups)


def group_sum_kernel(owner_ref, received_ref, out_ref, total):
    base = lax.axis_index("dp") * lax.axis_size("rollout")
    total[...] = jnp.zeros_like(total)
    for r in range(received_ref.shape[0]):
        total[owner_ref[base + r]] += received_ref[r].astype(F32)
    out_ref[...] = total[...].astype(out_ref.dtype)


def group_sums(owner, received, groups):
    shape = (groups,) + received.shape[1:]
    return pl.pallas_call(
        group_sum_kernel,
        out_shape=jax.ShapeDtypeStruct(shape, BF16),
        in_specs=[pl.BlockSpec(memory_space=pltpu.SMEM), pl.BlockSpec(memory_space=pltpu.VMEM)],
        out_specs=pl.BlockSpec(memory_space=pltpu.VMEM),
        scratch_shapes=[pltpu.VMEM(shape, F32)],
        name="group_sums",
    )(owner, received)


def final_sum_kernel(parts_ref, keys_ref, values_ref):
    total = parts_ref[0].astype(F32)
    for r in range(1, parts_ref.shape[0]):
        total += parts_ref[r].astype(F32)
    keys_ref[0] = total[0]
    values_ref[0] = total[1]


def final_sums(parts):
    out = jax.ShapeDtypeStruct((1,) + parts.shape[2:], F32)
    return pl.pallas_call(
        final_sum_kernel,
        out_shape=(out, out),
        in_specs=[pl.BlockSpec(memory_space=pltpu.VMEM)],
        out_specs=[pl.BlockSpec(memory_space=pltpu.VMEM)] * 2,
        name="final_sums",
    )(parts)


def attend_kernel(
    lengths_ref, q_ref, g_ref, resp_k_ref, resp_v_ref, prompt_k_ref, prompt_v_ref,
    out_ref, dq_ref, d_resp_k_ref, d_resp_v_ref, d_prompt_ref,
    keys, values, keys_t, values_t, dk_sum, dv_sum, *, group,
):
    length = lengths_ref[here_of()]
    scale = HEAD_DIM ** (-0.5)
    block = q_ref.shape[1]
    slices = prompt_k_ref.shape[0]
    prompt_n = keys.shape[0] - block
    keys[:prompt_n] = prompt_k_ref[:, 0].reshape(prompt_n, HEAD_DIM)
    keys[prompt_n:] = resp_k_ref[0]
    values[:prompt_n] = prompt_v_ref[:, 0].reshape(prompt_n, HEAD_DIM)
    values[prompt_n:] = resp_v_ref[0]
    keys_t[...] = keys[...].T
    values_t[...] = values[...].T
    dk_sum[...] = jnp.zeros_like(dk_sum)
    dv_sum[...] = jnp.zeros_like(dv_sum)

    def tile(t):
        span = prompt_n + (t + 1) * ROWS
        old = span - ROWS
        rows = pl.ds(t * ROWS, ROWS)
        live = (lax.broadcasted_iota(jnp.int32, (ROWS, HEAD_DIM), 0) + t * ROWS < length).astype(F32)
        allowed = lax.broadcasted_iota(jnp.int32, (ROWS, ROWS), 0) <= lax.broadcasted_iota(
            jnp.int32, (ROWS, ROWS), 1
        )
        for h in range(group):
            cols = pl.ds(h * HEAD_DIM, HEAD_DIM)
            q = q_ref[0, rows, cols]
            g_wide = g_ref[0, rows, cols].astype(F32) * live
            g = g_wide.astype(BF16)
            scores = lax.dot_general(keys[:span], q, ROW_BY_ROW, preferred_element_type=F32)
            dprobs = lax.dot_general(values[:span], g, ROW_BY_ROW, preferred_element_type=F32)
            scores = jnp.concatenate([scores[:old], jnp.where(allowed, scores[old:], -1e30)], axis=0)
            top = jnp.max(scores, axis=0, keepdims=True)
            probs = jnp.exp2((scores - top) * (scale * LOG2_E))
            probs = probs * (1.0 / jnp.sum(probs, axis=0, keepdims=True))
            weights = probs.astype(BF16)
            out_t = jnp.dot(values_t[:, :span], weights, preferred_element_type=F32)
            delta = jnp.sum(g_wide.T * out_t, axis=0, keepdims=True)
            dscores = (probs * (dprobs - delta) * scale).astype(BF16)
            dq_t = jnp.dot(keys_t[:, :span], dscores, preferred_element_type=F32)
            dk_sum[:span] += jnp.dot(dscores, q, preferred_element_type=F32)
            dv_sum[:span] += jnp.dot(weights, g, preferred_element_type=F32)
            out_ref[0, rows, cols] = (out_t.T * live).astype(BF16)
            dq_ref[0, rows, cols] = dq_t.T.astype(BF16)

    for t in range(block // ROWS):

        @pl.when(length > t * ROWS)
        def _():
            tile(t)

        @pl.when(length <= t * ROWS)
        def _():
            dead = jnp.zeros((ROWS, out_ref.shape[2]), BF16)
            out_ref[0, pl.ds(t * ROWS, ROWS)] = dead
            dq_ref[0, pl.ds(t * ROWS, ROWS)] = dead

    d_resp_k_ref[0] = dk_sum[prompt_n:].astype(BF16)
    d_resp_v_ref[0] = dv_sum[prompt_n:].astype(BF16)
    d_prompt_ref[:, 0] = dk_sum[:prompt_n].astype(BF16).reshape(slices, prompt_n // slices, HEAD_DIM)
    d_prompt_ref[:, 1] = dv_sum[:prompt_n].astype(BF16).reshape(slices, prompt_n // slices, HEAD_DIM)


def attend(lengths, q, g, resp_k, resp_v, prompt):
    block = q.shape[1]
    kv_heads = resp_k.shape[2] // HEAD_DIM
    group = q.shape[2] // resp_k.shape[2]
    slices, _, slice_rows, _ = prompt.shape
    span = slices * slice_rows + block
    wide = pl.BlockSpec((1, block, group * HEAD_DIM), lambda e, n: (0, 0, e))
    narrow = pl.BlockSpec((1, block, HEAD_DIM), lambda e, n: (0, 0, e))
    prompt_keys = pl.BlockSpec((slices, 1, slice_rows, HEAD_DIM), lambda e, n: (0, 0, 0, e))
    prompt_values = pl.BlockSpec((slices, 1, slice_rows, HEAD_DIM), lambda e, n: (0, 1, 0, e))
    both = pl.BlockSpec((slices, 2, slice_rows, HEAD_DIM), lambda e, n: (0, 0, 0, e))
    like = lambda x: jax.ShapeDtypeStruct(x.shape, BF16)
    return pl.pallas_call(
        functools.partial(attend_kernel, group=group),
        out_shape=(like(q), like(q), like(resp_k), like(resp_k), like(prompt)),
        grid_spec=pltpu.PrefetchScalarGridSpec(
            num_scalar_prefetch=1,
            grid=(kv_heads,),
            in_specs=[wide, wide, narrow, narrow, prompt_keys, prompt_values],
            out_specs=[wide, wide, narrow, narrow, both],
            scratch_shapes=[pltpu.VMEM((span, HEAD_DIM), BF16)] * 2
            + [pltpu.VMEM((HEAD_DIM, span), BF16)] * 2
            + [pltpu.VMEM((span, HEAD_DIM), F32)] * 2,
        ),
        compiler_params=pltpu.CompilerParams(vmem_limit_bytes=56 << 20),
        name="attend",
    )(lengths, q, g, resp_k, resp_v, prompt, prompt)


def exchange(pieces, axis):
    return lax.all_to_all(pieces, axis, split_axis=0, concat_axis=0, tiled=True)


def per_device(queries, resp_keys, resp_values, prompt_keys, prompt_values, d_out, lengths, owner):
    rollout_count = lax.axis_size("rollout")
    groups = lax.axis_size("dp")
    local = jnp.concatenate([prompt_keys, prompt_values], axis=0)
    every_group = exchange(jnp.broadcast_to(local[None], (groups,) + local.shape), "dp")
    prompt = exchange(select_slices(owner, every_group, rollout_count), "rollout")
    out, dq, dk, dv, d_prompt = attend(lengths, queries, d_out, resp_keys, resp_values, prompt)
    received = exchange(d_prompt, "rollout")
    parts = exchange(group_sums(owner, received, groups), "dp")
    d_prompt_keys, d_prompt_values = final_sums(parts)
    return out, dq, dk, dv, d_prompt_keys, d_prompt_values


def solution(mesh):
    by_block = P(("dp", "rollout"), None, None)
    by_prompt = P("dp", "rollout", None)
    return jax.shard_map(
        per_device,
        mesh=mesh,
        in_specs=(by_block, by_block, by_block, by_prompt, by_prompt, by_block, P(), P()),
        out_specs=(by_block, by_block, by_block, by_block, by_prompt, by_prompt),
        check_vma=False,
    )
```

time: 224 us -> 107 us (0.48)
  blocking collectives: 0 us -> 78.8 us
  waiting for transfers between devices: 72.4 us -> 0 us
  matrix products: 52.5 us -> 0 us
  local copies, waits for them, and re-layouts: 42.1 us -> 0.02 us
  other arithmetic: 29.7 us -> 0.74 us
  Pallas kernels: 0 us -> 26.6 us
  between operations: 16.9 us -> 0.64 us
  starting transfers between devices: 8.94 us -> 0 us
    all_to_all x0 -> x4, blocking collectives: none -> 78.8 us  [exchange(): return lax.all_to_all(pieces, axis, split_axis=0, concat_axis=0, tiled=True)]
    all_gather x1 -> x0, waiting for transfers between devices: 57.5 us -> none  [per_device(): gathered = lax.all_gather(local_pair, ('dp', 'rollout'), axis=0, tiled=True)]
    dot_general x25 -> x0, matrix products: 52.5 us -> none  [the longest x4 14.9 us: step(): jnp.einsum('kgts,skd->tkgd', dscore, key_heads, preferred_element_type=jn...]
    pallas_call x0 -> x4, Pallas kernels: none -> 26.6 us  [the longest x1 21.2 us: attend(): pl.pallas_call(functools.partial(attend_kernel, group=group), out_shape=(...]
    all_to_all x2 -> x0, waiting for transfers between devices: 14.9 us -> none  [the longest x1 10.4 us: per_device(): lax.all_to_all(pieces.astype(jnp.bfloat16), 'rollout', split_axis=1, conc...]
    sub x8 -> x0, other arithmetic: 14.8 us -> none  [the longest x4 14.7 us: step(): expd = jnp.exp(scores - top)]
    unnamed x16 -> x0, local copies, waits for them, and re-layouts: 13.2 us -> none
    dynamic_update_slice x16 -> x0, local copies, waits for them, and re-layouts: 9.02 us -> none  [the longest x8 4.53 us: step(): lax.dynamic_update_slice_in_dim(dq_all, dq.reshape(TILE, -1).astype(jnp.b...]
  transfers between devices with their start and end apart: 3 -> 0, of which waited for: 3 -> 0; matrix products, arithmetic and copies ran while one was open for 7% -> 0% of each run, Pallas kernels for 0% -> 0%
where the time goes in v1:
time: 107 us
  blocking collectives  78.8 us (74%)
  Pallas kernels  26.6 us (25%)
    all_to_all x4, blocking collectives, exchange(): return lax.all_to_all(pieces, axis, split_axis=0, concat_axis=0, tiled=True)  78.8 us
    pallas_call x1, Pallas kernels, attend(): pl.pallas_call(functools.partial(attend_kernel, group=group), out_shape=(...  21.2 us

profile of v1, /device:TPU:1, one launch (start us, length us, event | category | flops | bytes accessed | tf_op | source)
XLA Modules:
  0.0 106.7 jit_solution(17729613220896526866)
XLA Ops:
  0.6 0.7 pad_maximum_fusion
  1.4 12.2 %all_to_all.20.groups_ref = bf16[8,2,16,512]{3,2,1,0:T(8,128)(2,1)} all-to-all(bf16[8,2,16,512]{3,2,1,0:T(8,128)(2,1)S(1)} %broadcast_in_dim.2), channel_id=1, replica_groups=mesh['dp'=8,'rollout'=16] {'dp'}, dimensions={0} | all-to-all | bytes 524288 | tf_op jit(solution)/shard_map/all_to_all | solution.py:173
  13.6 1.8 %select_slices.1 = bf16[16,2,16,512]{3,2,1,0:T(8,128)(2,1)} custom-call(s32[128]{0:T(128)} %owner_ref.3, bf16[8,2,16,512]{3,2,1,0:T(8,128)(2,1)} %all_to_all.20.groups_ref), custom_call_target="tpu_custom_call" | custom-call | tf_op jit(solution)/shard_map/select_slices/pallas_call | solution.py:29
  15.4 17.8 %all_to_all.21.prompt_k_ref.prompt_v_ref = bf16[16,2,16,512]{3,2,1,0:T(8,128)(2,1)} all-to-all(bf16[16,2,16,512]{3,2,1,0:T(8,128)(2,1)} %select_slices.1), channel_id=1, replica_groups=mesh['dp'=8,'rollout'=16] {'rollout'}, dimensions={0} | all-to-all | bytes 1048576 | tf_op jit(solution)/shard_map/all_to_all | solution.py:173
  33.1 21.2 %attend.1 = (bf16[1,512,2560]{2,1,0:T(8,128)(2,1)}, bf16[1,512,2560]{2,1,0:T(8,128)(2,1)}, bf16[1,512,512]{2,1,0:T(8,128)(2,1)}, bf16[1,512,512]{2,1,0:T(8,128)(2,1)}, bf16[16,2,16,512]{3,2,1,0:T(8,128)(2,1)}) custom-call(s32[128]{0:T(128)} %lengths_ref.1, bf16[1,512,2560]{2,1,0:T(8,128)(2,1)} %q_ref.1, bf16[1,512,2560]{2,1,0:T(8,128)(2,1)} %g_ref.1, ...), custom_call_target="tpu_custom_call" | custom-call | tf_op jit(solution)/shard_map/attend/pallas_call | solution.py:155
  54.4 34.1 %all_to_all.22.received_ref = bf16[16,2,16,512]{3,2,1,0:T(8,128)(2,1)} all-to-all(bf16[16,2,16,512]{3,2,1,0:T(8,128)(2,1)} %get-tuple-element.17), channel_id=1, replica_groups=mesh['dp'=8,'rollout'=16] {'rollout'}, dimensions={0} | all-to-all | bytes 1048576 | tf_op jit(solution)/shard_map/all_to_all | solution.py:173
  88.5 1.9 %group_sums.1 = bf16[8,2,16,512]{3,2,1,0:T(8,128)(2,1)} custom-call(s32[128]{0:T(128)} %owner_ref.3, bf16[16,2,16,512]{3,2,1,0:T(8,128)(2,1)} %all_to_all.22.received_ref), custom_call_target="tpu_custom_call" | custom-call | tf_op jit(solution)/shard_map/group_sums/pallas_call | solution.py:48
  90.4 14.7 %all_to_all.23.parts_ref = bf16[8,2,16,512]{3,2,1,0:T(8,128)(2,1)} all-to-all(bf16[8,2,16,512]{3,2,1,0:T(8,128)(2,1)} %group_sums.1), channel_id=1, replica_groups=mesh['dp'=8,'rollout'=16] {'dp'}, dimensions={0} | all-to-all | bytes 524288 | tf_op jit(solution)/shard_map/all_to_all | solution.py:173
  105.1 1.6 %final_sums.1 = (f32[1,16,512]{2,1,0:T(8,128)}, f32[1,16,512]{2,1,0:T(8,128)}) custom-call(bf16[8,2,16,512]{3,2,1,0:T(8,128)(2,1)} %all_to_all.23.parts_ref), custom_call_target="tpu_custom_call" | custom-call | tf_op jit(solution)/shard_map/final_sums/pallas_call | solution.py:68
  (1 shorter events, 0.0 us)
